TPU v7x, 32 devices: a whole 2x2x4 slice. The times are simulated.
32 devices in a mesh: grp: 4 (over x, core), blk: 2 (over y), set: 4 (over z).
Axes of the slice: x: 2, y: 2, z: 4, core: 2. Of those that a mesh axis runs over, the one named last changes fastest.
Arguments:
- queries: bfloat16 [4096, 384], P(('grp', 'blk', 'set')), may hold values from -8 to 8
- keys: bfloat16 [4096, 384], P(('grp', 'blk', 'set')), may hold values from -8 to 8
- values: bfloat16 [4096, 384], P(('grp', 'blk', 'set')), may hold values from -6 to 6
- valid: int32 [4096], P(('grp', 'blk', 'set')), may hold values 0 or 1
- offsets: int32 [2, 6], replicated, may hold values from 0 to 7, as said below
- w_out: bfloat16 [384, 768], replicated, may hold values from -0.3125 to 0.3125
Outputs:
- projected: bfloat16 [4096, 768], P(('grp', 'blk', 'set'))
Inputs may be any that keep to these rules, and one draw needn't show every extreme that they name: offsets[0, h] lies in 0 to 1 and offsets[1, h] - offsets[0, h] is a multiple of 2 for every head h.
All inputs are finite; a program needn't handle non-finite values. No bound on the sum of `valid` on one device may be relied on, other than what follows from the above.
Results may differ from a plain program's by a relative error of at most 0.0015.
The roundings to bfloat16 on the way count: a program that leaves them out, or rounds other values in their place, can miss the bound.
Values may be sent and summed in bfloat16 or wider, within the bound.
A program may use at most 64 MiB of HBM per device.

v0:
```python
import math

import jax
import jax.numpy as jnp
from jax import lax
from jax.sharding import PartitionSpec as P

HEAD_COUNT = 6
HD = 64


def head_attend(query_head, key_head, value_head, key_allowed, self_slot, scaling):
    scores = (
        lax.dot_general(
            query_head, key_head, (((1,), (1,)), ((), ())), preferred_element_type=jnp.float32
        )
        * scaling
    )
    columns = jnp.arange(key_head.shape[0], dtype=jnp.int32)
    allowed = key_allowed[None, :] | (columns[None, :] == self_slot[:, None])
    scores = jnp.where(allowed, scores, jnp.float32(-1e30))
    highest = jnp.max(scores, axis=1, keepdims=True)
    weights = jnp.exp(scores - highest)
    totals = jnp.sum(weights, axis=1)
    mixture = (
        jnp.dot(weights.astype(jnp.bfloat16), value_head, preferred_element_type=jnp.float32)
        / totals[:, None]
    )
    return (mixture, highest[:, 0] + jnp.log(totals))


def attend(queries, keys, values, key_allowed, self_slot):
    row_count = queries.shape[0]
    length = keys.shape[0]
    heads_query = queries.reshape(row_count, HEAD_COUNT, HD).transpose(1, 0, 2)
    heads_key = keys.reshape(length, HEAD_COUNT, HD).transpose(1, 0, 2)
    heads_value = values.reshape(length, HEAD_COUNT, HD).transpose(1, 0, 2)
    scaling = 1.0 / math.sqrt(HD)
    mixture, log_totals = lax.map(
        lambda packed: head_attend(packed[0], packed[1], packed[2], packed[3], self_slot, scaling),
        (heads_query, heads_key, heads_value, key_allowed.T),
    )
    return (mixture.transpose(1, 0, 2).reshape(row_count, HEAD_COUNT * HD), log_totals.T)


def selector_table(shift_amount, cycle_length):
    return jnp.arange(cycle_length, dtype=jnp.int32)[:, None] == shift_amount[None, :]


def pick_rows(matrix, shift_amount, cycle_length):
    row_total = matrix.shape[0]
    selector = selector_table(shift_amount, cycle_length)
    blocks = matrix.reshape(row_total // cycle_length, cycle_length, HEAD_COUNT, HD)
    chosen = jnp.sum(
        jnp.where(selector[None, :, :, None], blocks, jnp.zeros((), matrix.dtype)), axis=1
    )
    return chosen.reshape(row_total // cycle_length, HEAD_COUNT * HD)


def pick_flags(key_flags, shift_amount, cycle_length):
    row_total = key_flags.shape[0]
    selector = selector_table(shift_amount, cycle_length)
    blocks = key_flags.reshape(row_total // cycle_length, cycle_length)
    return jnp.sum(
        jnp.where(selector[None, :, :], blocks[:, :, None], jnp.zeros((), key_flags.dtype)), axis=1
    )


def pick_head_flags(head_flags, shift_amount, cycle_length):
    row_total = head_flags.shape[0]
    selector = selector_table(shift_amount, cycle_length)
    blocks = head_flags.reshape(row_total // cycle_length, cycle_length, HEAD_COUNT)
    return jnp.sum(jnp.where(selector[None, :, :], blocks, jnp.zeros((), head_flags.dtype)), axis=1)


def spread_back(mixture, log_totals, shift_amount, cycle_length):
    row_count = mixture.shape[0]
    selector = selector_table(shift_amount, cycle_length)
    wide = jnp.where(
        selector[None, :, :, None], mixture.reshape(row_count, 1, HEAD_COUNT, HD), jnp.float32(0.0)
    )
    spread_totals = jnp.where(selector[None, :, :], log_totals[:, None, :], jnp.float32(0.0))
    present = jnp.broadcast_to(selector[None, :, :], (row_count, cycle_length, HEAD_COUNT))
    return (
        wide.reshape(row_count * cycle_length, HEAD_COUNT * HD),
        spread_totals.reshape(row_count * cycle_length, HEAD_COUNT),
        present.reshape(row_count * cycle_length, HEAD_COUNT),
    )


def combine(levels):
    highest = levels[0][1]
    for entry in levels[1:]:
        highest = jnp.maximum(highest, jnp.where(entry[2], entry[1], highest))
    numerator = jnp.zeros(levels[0][0].shape, jnp.float32)
    denominator = jnp.zeros(levels[0][1].shape, jnp.float32)
    for entry in levels:
        scaled = jnp.where(entry[2], jnp.exp(entry[1] - highest), jnp.float32(0.0))
        expanded = jnp.broadcast_to(scaled[:, :, None], (scaled.shape[0], HEAD_COUNT, HD)).reshape(
            scaled.shape[0], HEAD_COUNT * HD
        )
        numerator = numerator + entry[0] * expanded
        denominator = denominator + scaled
    wide_denominator = jnp.broadcast_to(
        denominator[:, :, None], (denominator.shape[0], HEAD_COUNT, HD)
    ).reshape(denominator.shape[0], HEAD_COUNT * HD)
    return numerator / wide_denominator


def per_device(queries, keys, values, valid, offsets, w_out):
    row_count = queries.shape[0]
    inner_size = lax.axis_size("set")
    block_size = lax.axis_size("blk")
    group_size = lax.axis_size("grp")
    inner_index = lax.axis_index("set")
    block_index = lax.axis_index("blk")
    group_index = lax.axis_index("grp")
    outer_period = block_size * group_size
    key_flags = valid.astype(jnp.bfloat16)
    dense_keys, dense_values, dense_flags = (
        lax.all_gather(keys, "set", axis=0, tiled=True),
        lax.all_gather(values, "set", axis=0, tiled=True),
        lax.all_gather(key_flags, "set", axis=0, tiled=True),
    )
    segment_rows = dense_keys.shape[0]
    dense_allowed = jnp.broadcast_to((dense_flags > 0)[:, None], (segment_rows, HEAD_COUNT))
    own_slots = inner_index * row_count + jnp.arange(row_count, dtype=jnp.int32)
    dense_level = attend(queries, dense_keys, dense_values, dense_allowed, own_slots)
    middle_shift = offsets[0]
    outer_shift = offsets[1]
    middle_key_part = pick_rows(dense_keys, middle_shift, block_size)
    middle_value_part = pick_rows(dense_values, middle_shift, block_size)
    middle_flag_part = pick_flags(dense_flags, middle_shift, block_size)
    middle_keys, middle_values, middle_flags = (
        lax.all_gather(middle_key_part, "blk", axis=0, tiled=True),
        lax.all_gather(middle_value_part, "blk", axis=0, tiled=True),
        lax.all_gather(middle_flag_part, "blk", axis=0, tiled=True),
    )
    stride_offset = (outer_shift - middle_shift) // block_size
    outer_key_part = pick_rows(middle_keys, stride_offset, group_size)
    outer_value_part = pick_rows(middle_values, stride_offset, group_size)
    outer_flag_part = pick_head_flags(middle_flags, stride_offset, group_size)
    outer_keys, outer_values, outer_flags = (
        lax.all_gather(outer_key_part, "grp", axis=0, tiled=True),
        lax.all_gather(outer_value_part, "grp", axis=0, tiled=True),
        lax.all_gather(outer_flag_part, "grp", axis=0, tiled=True),
    )
    middle_count = row_count // block_size
    middle_slots = (block_index * inner_size + inner_index) * middle_count + jnp.arange(
        middle_count, dtype=jnp.int32
    )
    middle_level = attend(
        pick_rows(queries, middle_shift, block_size),
        middle_keys,
        middle_values,
        middle_flags > 0,
        middle_slots,
    )
    outer_count = row_count // outer_period
    outer_slots = (
        (group_index * block_size + block_index) * inner_size + inner_index
    ) * outer_count + jnp.arange(outer_count, dtype=jnp.int32)
    outer_level = attend(
        pick_rows(queries, outer_shift, outer_period),
        outer_keys,
        outer_values,
        outer_flags > 0,
        outer_slots,
    )
    levels = [
        (dense_level[0], dense_level[1], jnp.ones((row_count, HEAD_COUNT), jnp.bool_)),
        spread_back(middle_level[0], middle_level[1], middle_shift, block_size),
        spread_back(outer_level[0], outer_level[1], outer_shift, outer_period),
    ]
    attention = combine(levels).astype(jnp.bfloat16)
    return jnp.dot(attention, w_out, preferred_element_type=jnp.float32).astype(jnp.bfloat16)


def solution(mesh):
    in_specs = (
        P(("grp", "blk", "set"), None),
        P(("grp", "blk", "set"), None),
        P(("grp", "blk", "set"), None),
        P(("grp", "blk", "set")),
        P(),
        P(),
    )
    out_specs = P(("grp", "blk", "set"), None)
    return jax.shard_map(
        per_device, mesh=mesh, in_specs=in_specs, out_specs=out_specs, check_vma=False
    )
```

profile of v0, /device:TPU:0, one launch (start us, length us, event | category | flops | bytes accessed | tf_op | source)
XLA Modules:
  0.0 111.3 jit_solution(5796271191207489158)
XLA Ops:
  0.0 0.7 copy-done.13
  0.7 12.6 %all-gather = bf16[4,1,128]{2,1,0:T(2,128)(2,1)S(1)} all-gather(bf16[1,1,128]{2,1,0:T(2,128)(2,1)S(1)} %convert_bitcast_fusion), channel_id=1, replica_groups=mesh['grp'=4,'blk'=2,'set'=4] {'set'}, dimensions={0}, use_global_device_ids=true | all-gather | bytes 1280 | tf_op jit(solution)/shard_map/all_gather | solution.py:123
  13.4 0.7 copy-done.11
  14.3 0.7 copy.112
  15.1 0.7 reshape.303
  15.8 0.7 reshape.295
  16.9 4.4 %all_gather.30 = bf16[512,6]{0,1:T(8,128)(2,1)S(1)} all-gather(bf16[256,6]{0,1:T(8,128)(2,1)S(1)} %fusion.57), channel_id=1, replica_groups=mesh['grp'=4,'blk'=2,'set'=4] {'blk'}, dimensions={0}, use_global_device_ids=true | all-gather | bytes 9216 | tf_op jit(solution)/shard_map/all_gather | solution.py:137
  21.4 0.8 copy-done.6
  22.3 0.8 copy-done.2
  23.2 0.4 reshape.304
  23.8 5.2 %all_gather.33 = bf16[512,6]{0,1:T(8,128)(2,1)S(1)} all-gather(bf16[128,6]{0,1:T(8,128)(2,1)S(1)} %select_reduce_fusion.6), channel_id=1, replica_groups=mesh['grp'=4,'blk'=2,'set'=4] {'grp'}, dimensions={0}, use_global_device_ids=true | all-gather | bytes 7680 | tf_op jit(solution)/shard_map/all_gather | solution.py:146
  29.7 14.4 %all_gather.29 = bf16[512,384]{0,1:T(8,128)(2,1)S(1)} all-gather(bf16[128,384]{0,1:T(8,128)(2,1)S(1)} %copy.95), channel_id=1, replica_groups=mesh['grp'=4,'blk'=2,'set'=4] {'set'}, dimensions={0}, use_global_device_ids=true | all-gather | bytes 491520 | tf_op jit(solution)/shard_map/all_gather | solution.py:122
  44.1 13.3 %all_gather.28 = bf16[512,384]{0,1:T(8,128)(2,1)S(1)} all-gather(bf16[128,384]{0,1:T(8,128)(2,1)S(1)} %copy.94), channel_id=1, replica_groups=mesh['grp'=4,'blk'=2,'set'=4] {'set'}, dimensions={0}, use_global_device_ids=true | all-gather | bytes 491520 | tf_op jit(solution)/shard_map/all_gather | solution.py:121
  57.4 5.2 %while.39 = (s32[]{:T(128)}, f32[6,128,64]{1,2,0:T(8,128)S(1)}, f32[6,128]{1,0:T(8,128)S(1)}, pred[6,512]{1,0:T(8,128)(4,1)S(1)}, bf16[6,128,64]{1,2,0:T(8,128)(...) while((s32[]{:T(128)}, f32[6,128,64]{1,2,0:T(8,128)S(1)}, ...), condition=%wide.region_3.4_spmd.clone, body=%wide.region_0.3_spmd.clone.sunk | while | flops 17375232 | bytes 976505 | solution.py:39
  57.5 0.3 fusion.83
  58.0 0.3 fusion.85
  58.3 0.3 fusion.83
  58.9 0.3 fusion.85
  59.2 0.3 fusion.83
  59.7 0.3 fusion.85
  60.1 0.3 fusion.83
  60.6 0.3 fusion.85
  60.9 0.3 fusion.83
  61.4 0.3 fusion.85
  61.8 0.3 fusion.83
  62.3 0.3 fusion.85
  62.6 0.9 copy.102
  63.8 0.6 reshape.300
  64.3 0.4 copy-done.1
  64.8 0.6 reshape.297
  65.3 1.6 %select_reduce_fusion.2 = (bf16[256,6,64]{2,1,0:T(8,128)(2,1)}, bf16[256,6,64]{2,1,0:T(8,128)(2,1)S(1)}) fusion(bf16[256,2,6,64]{3,2,1,0:T(8,128)(2,1)S(1)} %reshape.300, pred[2,6]{1,0:T(4,128)(4,1)S(1)} %iota_compare_fusion.5, bf16[256,2,6,64]{3,2,1,0:T(8,128)(2,1)S(1)} %reshape.297), kind=kLoop, calls=%fused_computation.72 | loop fusion | flops 589824 | bytes 1179660 | tf_op jit(solution)/shard_map/reduce_sum | solution.py:54
  66.9 1.3 %copy.105 = bf16[256,6,64]{0,2,1:T(8,128)(2,1)S(1)} copy(bf16[256,6,64]{2,1,0:T(8,128)(2,1)} %get-tuple-element.295) | data formatting | bytes 393216 | tf_op jit(solution)/shard_map/reduce_sum | solution.py:54
  68.2 8.2 %all_gather.32 = bf16[512,384]{0,1:T(8,128)(2,1)S(1)} all-gather(bf16[256,384]{0,1:T(8,128)(2,1)S(1)} %bitcast.192), channel_id=1, replica_groups=mesh['grp'=4,'blk'=2,'set'=4] {'blk'}, dimensions={0}, use_global_device_ids=true | all-gather | bytes 589824 | tf_op jit(solution)/shard_map/all_gather | solution.py:136
  76.4 0.3 copy.103
  76.7 6.3 %all_gather.31 = bf16[512,384]{0,1:T(8,128)(2,1)S(1)} all-gather(bf16[256,384]{0,1:T(8,128)(2,1)S(1)} %bitcast.193), channel_id=1, replica_groups=mesh['grp'=4,'blk'=2,'set'=4] {'blk'}, dimensions={0}, use_global_device_ids=true | all-gather | bytes 589824 | tf_op jit(solution)/shard_map/all_gather | solution.py:135
  83.1 4.6 %while.40 = (s32[]{:T(128)}, f32[6,64,64]{2,1,0:T(8,128)S(1)}, f32[6,64]{1,0:T(8,128)S(1)}, pred[6,512]{1,0:T(8,128)(4,1)S(1)}, bf16[6,64,64]{2,1,0:T(8,128)(2,1...) while((s32[]{:T(128)}, f32[6,64,64]{2,1,0:T(8,128)S(1)}, ...), condition=%wide.region_11.12_spmd.clone, body=%wide.region_8.11_spmd.clone.sunk | while | flops 8687618 | bytes 580985 | solution.py:39
  83.9 0.3 fusion.88
  84.6 0.3 fusion.88
  85.4 0.3 fusion.88
  86.2 0.3 fusion.88
  88.8 0.6 reshape.309
  89.4 0.6 reshape.306
  90.0 0.9 select_reduce_fusion
  91.3 6.5 %all_gather.34 = bf16[512,384]{0,1:T(8,128)(2,1)S(1)} all-gather(bf16[128,384]{0,1:T(8,128)(2,1)S(1)} %bitcast.197), channel_id=1, replica_groups=mesh['grp'=4,'blk'=2,'set'=4] {'grp'}, dimensions={0}, use_global_device_ids=true | all-gather | bytes 491520 | tf_op jit(solution)/shard_map/all_gather | solution.py:144
  97.8 6.7 %all_gather.35 = bf16[512,384]{0,1:T(8,128)(2,1)S(1)} all-gather(bf16[128,384]{0,1:T(8,128)(2,1)S(1)} %bitcast.196), channel_id=1, replica_groups=mesh['grp'=4,'blk'=2,'set'=4] {'grp'}, dimensions={0}, use_global_device_ids=true | all-gather | bytes 491520 | tf_op jit(solution)/shard_map/all_gather | solution.py:145
  104.6 4.3 %while.41 = (s32[]{:T(128)}, f32[6,16,64]{2,1,0:T(8,128)S(1)}, f32[6,16]{1,0:T(8,128)S(1)}, pred[6,512]{1,0:T(8,128)(4,1)S(1)}, bf16[6,16,64]{2,1,0:T(8,128)(2,1...) while((s32[]{:T(128)}, f32[6,16,64]{2,1,0:T(8,128)S(1)}, ...), condition=%wide.region_19.20_spmd.clone, body=%wide.region_16.19_spmd.clone.sunk | while | flops 2171906 | bytes 247481 | solution.py:39
  109.1 0.6 copy-done.8
  110.3 1.0 convolution_convert_fusion
  (186 shorter events, 13.8 us)
Async XLA Ops:
  0.0 110.3 %copy-start = (bf16[384,768]{1,0:T(8,128)(2,1)S(1)}, bf16[384,768]{1,0:T(8,128)(2,1)}, u32[]{:S(2)}) copy-start(bf16[384,768]{1,0:T(8,128)(2,1)} %param.17) | copy-start | bytes 1769476
  0.0 0.7 copy-start.13
  13.4 0.7 copy-start.11
  15.8 5.5 %copy-start.5 = (bf16[128,384]{1,0:T(8,128)(2,1)S(1)}, bf16[128,384]{1,0:T(8,128)(2,1)}, u32[]{:S(2)}) copy-start(bf16[128,384]{1,0:T(8,128)(2,1)} %param.13) | copy-start | bytes 294916
  21.3 0.9 copy-start.6
  22.2 0.9 copy-start.2
  62.6 0.9 copy-start.3
  63.8 1.0 copy-start.1
  89.4 0.7 copy-start.12
  97.8 6.7 %copy-start.7 = (f32[6,16,64]{2,1,0:T(8,128)S(1)}, f32[6,16,64]{2,1,0:T(8,128)}, u32[]{:S(2)}) copy-start(f32[6,16,64]{2,1,0:T(8,128)} %custom-call.4) | copy-start | bytes 73732
  97.8 6.7 %copy-start.10 = (f32[6,16]{1,0:T(8,128)S(1)}, f32[6,16]{1,0:T(8,128)}, u32[]{:S(2)}) copy-start(f32[6,16]{1,0:T(8,128)} %custom-call.5) | copy-start | bytes 1156
  108.9 0.9 copy-start.4
  109.0 0.7 copy-start.8
  109.0 0.7 copy-start.9
where the time goes:
time: 112 us; the launch traced here: 111 us
  blocking collectives  77.7 us (69%)
  local copies, waits for them, and re-layouts  15.7 us (14%)
  matrix products  9.82 us (9%)
  other arithmetic  7.34 us (7%)
    all_gather x1, blocking collectives, per_device(): lax.all_gather(values, 'set', axis=0, tiled=True)  14.4 us
    all_gather x1, blocking collectives, per_device(): lax.all_gather(keys, 'set', axis=0, tiled=True)  13.3 us
    all_gather x1, blocking collectives, per_device(): lax.all_gather(key_flags, 'set', axis=0, tiled=True)  12.6 us
    all_gather x1, blocking collectives, per_device(): lax.all_gather(middle_value_part, 'blk', axis=0, tiled=True)  8.21 us
    all_gather x1, blocking collectives, per_device(): lax.all_gather(outer_value_part, 'grp', axis=0, tiled=True)  6.72 us
    all_gather x1, blocking collectives, per_device(): lax.all_gather(outer_key_part, 'grp', axis=0, tiled=True)  6.5 us
    all_gather x1, blocking collectives, per_device(): lax.all_gather(middle_key_part, 'blk', axis=0, tiled=True)  6.34 us
    all_gather x1, blocking collectives, per_device(): lax.all_gather(outer_flag_part, 'grp', axis=0, tiled=True)  5.19 us

commit v1 on v0

v1 whole, which is shorter than its diff:
```python
import functools

import jax
import jax.numpy as jnp
from jax import lax
from jax.experimental import pallas as pl
from jax.experimental.pallas import tpu as pltpu
from jax.sharding import PartitionSpec as P

HEAD_COUNT = 6
HD = 64
LANES = 128
UNIT = 16
FLAG_STRIDE = 8
CHUNKS = HEAD_COUNT * HD // LANES
MESH = pl.DeviceIdType.MESH
NEG = -1e30


def units(count):
    return -(-count // UNIT)


def split_pow2(x, size):
    shift = size.bit_length() - 1
    return lax.shift_right_logical(x, shift), x & (size - 1)


class Plan:
    def __init__(self, grp, blk, n, rows):
        self.grp, self.blk, self.n, self.rows = grp, blk, n, rows
        self.period = grp * blk
        self.c3 = rows // self.period
        c2 = rows // blk
        self.counts = (self.c3, c2 - self.c3, rows - c2)
        self.units = tuple(units(c) for c in self.counts)
        self.sizes = tuple(u * UNIT for u in self.units)
        self.starts = (0, self.sizes[0], self.sizes[0] + self.sizes[1])
        self.total = sum(self.sizes)

    def source(self, t):
        a = t
        b = t - self.starts[1]
        c = t - self.starts[2]
        bv, bg = split_pow2(b, self.c3)
        cv, cg = split_pow2(c, self.c3)
        ck, cm = split_pow2(cv, self.grp)
        is_a = t < self.starts[1]
        is_b = t < self.starts[2]
        group = jnp.where(is_a, a, jnp.where(is_b, bg, cg))
        slot = jnp.where(is_a, 0, jnp.where(is_b, (bv + 1) * self.blk, cm * self.blk + ck + 1))
        local = jnp.where(is_a, a, jnp.where(is_b, b, c))
        count = jnp.where(is_a, self.counts[0], jnp.where(is_b, self.counts[1], self.counts[2]))
        return jnp.where(local < count, group * self.period, -(1 << 20)), slot


def kernel(
    plan, q_ref, k_ref, v_ref, valid_ref, offs_ref, w_ref, o_ref,
    buf_a, buf_b, buf_c, qs, zrecv, zsend, yrecv, ysend, xrecv, xsend, fsend,
):
    G, B, N = plan.grp, plan.blk, plan.n
    R = plan.total
    gi, bi, si = lax.axis_index("grp"), lax.axis_index("blk"), lax.axis_index("set")
    core = gi % 2
    partner = gi + 1 - 2 * core

    def peer_grp(step):
        return lax.rem(gi + 2 * step, G)

    barrier = pltpu.get_barrier_semaphore()

    def greet(g, b, s):
        pl.semaphore_signal(barrier, inc=1, device_id=(g, b, s), device_id_type=MESH)

    @pl.when(si > 0)
    def _():
        greet(gi, bi, si - 1)

    @pl.when(si < N - 1)
    def _():
        greet(gi, bi, si + 1)

    for step in range(1, B):
        greet(gi, lax.rem(bi + step, B), si)
    for step in range(1, G // 2):
        greet(peer_grp(step), bi, si)
    greet(partner, bi, si)

    lane = lax.broadcasted_iota(jnp.int32, (R, LANES), 1)
    base, slot = plan.source(lax.broadcasted_iota(jnp.int32, (R, plan.rows), 0))
    token = lax.broadcasted_iota(jnp.int32, (R, plan.rows), 1)
    valid_row = (valid_ref[...] > 0).astype(jnp.float32)
    flag_lane = lax.broadcasted_iota(jnp.int32, (UNIT, LANES), 1)
    flags = jnp.zeros((UNIT, LANES), jnp.float32)
    for c in range(CHUNKS):
        cols = slice(c * LANES, (c + 1) * LANES)
        packed = jnp.concatenate([q_ref[:, cols], k_ref[:, cols], v_ref[:, cols]], axis=1)
        moved = []
        for half in range(2):
            h = 2 * c + half
            hit = token == base + ((slot + offs_ref[1, h]) & (plan.period - 1))
            onehot = jnp.where(hit, jnp.float32(1), jnp.float32(0))
            moved.append(jnp.dot(onehot.astype(jnp.bfloat16), packed, preferred_element_type=jnp.float32))
            column = jnp.sum(onehot * valid_row, axis=1, keepdims=True)
            for u in range(R // UNIT):
                flags = jnp.where(
                    flag_lane == u * FLAG_STRIDE + h, column[u * UNIT:(u + 1) * UNIT, :], flags
                )
        for part in range(3):
            seg = slice(part * LANES, (part + 1) * LANES)
            got = jnp.where(lane < HD, moved[0][:, seg], moved[1][:, seg])
            if part == 0:
                qs[c] = (got * 0.125).astype(jnp.bfloat16)
                continue
            got = got.astype(jnp.bfloat16)
            at = c + (part - 1) * CHUNKS
            buf_a[0, 0, 0, at] = got[:plan.starts[1]]
            buf_b[0, 0, at] = got[plan.starts[1]:plan.starts[2]]
            buf_c[0, at] = got[plan.starts[2]:]
    buf_a[0, 0, 0, 2 * CHUNKS, 0:UNIT] = flags.astype(jnp.bfloat16)

    left_side = jnp.where(si > 0, 1, 0)
    right_side = jnp.where(si < N - 1, 1, 0)
    pl.semaphore_wait(barrier, left_side + right_side + (B - 1) + (G // 2 - 1) + 1)

    def zslot(part, r):
        return (buf_a.at[0, 0, r], buf_b.at[0, r], buf_c.at[r])[part]

    def zcopy(part, r, direction):
        to = (r + 1) % N if direction == 0 else (r - 1) % N
        near = si - 1 if direction == 0 else si + 1
        return pltpu.make_async_remote_copy(
            src_ref=zslot(part, r), dst_ref=zslot(part, to),
            send_sem=zsend.at[part, r, direction], recv_sem=zrecv.at[part, to],
            device_id=(gi, bi, near), device_id_type=MESH,
        )

    def ycopy(part, r, step):
        to = B - step

        def place(x):
            return buf_a.at[0, x, r] if part == 0 else buf_b.at[x, r]

        return pltpu.make_async_remote_copy(
            src_ref=place(0), dst_ref=place(to),
            send_sem=ysend.at[part, step, r], recv_sem=yrecv.at[part, to, r],
            device_id=(gi, lax.rem(bi + step, B), si), device_id_type=MESH,
        )

    def xcopy(y, r, step):
        to = (2 * (G // 2 - step)) % G
        return pltpu.make_async_remote_copy(
            src_ref=buf_a.at[0, y, r], dst_ref=buf_a.at[to, y, r],
            send_sem=xsend.at[step, y, r], recv_sem=xrecv.at[to, y, r],
            device_id=(peer_grp(step), bi, si), device_id_type=MESH,
        )

    def fcopy(x, y, r):
        return pltpu.make_async_remote_copy(
            src_ref=buf_a.at[x, y, r], dst_ref=buf_a.at[x + 1, y, r],
            send_sem=fsend.at[x, y, r], recv_sem=xrecv.at[x + 1, y, r],
            device_id=(partner, bi, si), device_id_type=MESH,
        )

    def spread_grp(y, r):
        for step in range(1, G // 2):
            xcopy(y, r, step).start()
        fcopy(0, y, r).start()

    def spread_blk(part, r):
        for step in range(1, B):
            ycopy(part, r, step).start()

    def own_z(part):
        @pl.when(si > 0)
        def _():
            zcopy(part, 0, 0).start()

        @pl.when(si < N - 1)
        def _():
            zcopy(part, 0, 1).start()

    def arrive(part, r):
        pltpu.make_async_copy(zslot(part, r), zslot(part, r), zrecv.at[part, r]).wait()

    def take(part, d):
        @pl.when(si + d <= N - 1)
        def _():
            arrive(part, d)

            @pl.when(si > 0)
            def _():
                zcopy(part, d, 0).start()

            if part < 2:
                spread_blk(part, d)
            if part == 0:
                spread_grp(0, d)

        @pl.when(si - d >= 0)
        def _():
            arrive(part, N - d)

            @pl.when(si < N - 1)
            def _():
                zcopy(part, N - d, 1).start()

            if part < 2:
                spread_blk(part, N - d)
            if part == 0:
                spread_grp(0, N - d)

    own_z(0)
    spread_blk(0, 0)
    spread_grp(0, 0)
    own_z(1)
    spread_blk(1, 0)
    for d in range(1, N):
        take(0, d)
        take(1, d)
        if d == 1:
            own_z(2)
    for r in range(N):
        for y in range(1, B):
            ref = buf_a.at[0, y, r]
            pltpu.make_async_copy(ref, ref, yrecv.at[0, y, r]).wait()
            spread_grp(y, r)
    if N > 1:
        take(2, 1)
    for r in range(N):
        for y in range(B):
            for step in range(1, G // 2):
                ref = buf_a.at[2 * step, y, r]
                pltpu.make_async_copy(ref, ref, xrecv.at[2 * step, y, r]).wait()
                fcopy(2 * step, y, r).start()
    for d in range(2, N):
        take(2, d)

    head_pick = lax.broadcasted_iota(jnp.int32, (FLAG_STRIDE, LANES), 1) & (FLAG_STRIDE - 1)
    head_pick = head_pick == lax.broadcasted_iota(jnp.int32, (FLAG_STRIDE, LANES), 0)
    head_pick = jnp.where(head_pick, jnp.float32(1), jnp.float32(0)).astype(jnp.bfloat16)

    def gather(level, at):
        pieces = []
        for u in range(plan.units[0]):
            rows = slice(u * UNIT, (u + 1) * UNIT)
            part = (buf_a[0, 0, :, at, rows], buf_a[0, :, :, at, rows], buf_a[:, :, :, at, rows])[level]
            pieces.append(part.reshape(-1, LANES))
        if level < 2:
            for u in range(plan.units[1]):
                rows = slice(u * UNIT, (u + 1) * UNIT)
                part = buf_b[0, :, at, rows] if level == 0 else buf_b[:, :, at, rows]
                pieces.append(part.reshape(-1, LANES))
        if level == 0:
            for u in range(plan.units[2]):
                pieces.append(buf_c[:, at, u * UNIT:(u + 1) * UNIT].reshape(-1, LANES))
        return pieces[0] if len(pieces) == 1 else jnp.concatenate(pieces, axis=0)

    def level_attend(level):
        M = (R, plan.starts[2], plan.starts[1])[level]
        tiles = M // UNIT
        devices = (N, B * N, G * B * N)[level]
        per_unit = devices * UNIT
        rows = slice(0, UNIT)
        at = 2 * CHUNKS
        tall = (buf_a[0, 0, :, at, rows], buf_a[0, :, :, at, rows], buf_a[:, :, :, at, rows])[level]
        tall = tall.reshape(per_unit, LANES).astype(jnp.float32)
        unit_lane = lax.broadcasted_iota(jnp.int32, (per_unit, LANES), 1) // FLAG_STRIDE
        tall = [jnp.where(unit_lane == u, tall, 0.0).astype(jnp.bfloat16) for u in range(tiles)]
        tall = tall[0] if tiles == 1 else jnp.concatenate(tall, axis=0)
        ok = lax.dot_general(
            head_pick, tall, (((1,), (1,)), ((), ())), preferred_element_type=jnp.float32
        )
        keys = per_unit * tiles
        t = lax.broadcasted_iota(jnp.int32, (M, keys), 0)
        own = lax.broadcasted_iota(jnp.int32, (M, keys), 1) == (t // UNIT) * per_unit + (t % UNIT)
        half_lane = lax.broadcasted_iota(jnp.int32, (M, LANES), 1) < HD
        results = []
        for c in range(CHUNKS):
            q = qs[c, 0:M]
            zero = jnp.zeros_like(q)
            both = jnp.concatenate([jnp.where(half_lane, q, zero), jnp.where(half_lane, zero, q)], axis=0)
            scores = lax.dot_general(
                both, gather(level, c), (((1,), (1,)), ((), ())), preferred_element_type=jnp.float32
            )
            values = gather(level, CHUNKS + c)
            probs, tops, totals = [], [], []
            for half in range(2):
                h = 2 * c + half
                s = jnp.where(own | (ok[h:h + 1, :] > 0.5), scores[half * M:(half + 1) * M], NEG)
                top = jnp.max(s, axis=1, keepdims=True)
                weight = jnp.exp(s - top)
                totals.append(jnp.sum(weight, axis=1, keepdims=True))
                tops.append(top)
                probs.append(weight.astype(jnp.bfloat16))
            mixed = jnp.dot(jnp.concatenate(probs, axis=0), values, preferred_element_type=jnp.float32)
            mixture = jnp.where(half_lane, mixed[:M] / totals[0], mixed[M:] / totals[1])
            lse = jnp.where(half_lane, tops[0] + jnp.log(totals[0]), tops[1] + jnp.log(totals[1]))
            results.append((mixture, lse))
        return results

    first = level_attend(0)
    for r in range(N):
        for y in range(1, B):
            ref = buf_b.at[y, r]
            pltpu.make_async_copy(ref, ref, yrecv.at[1, y, r]).wait()
    second = level_attend(1)
    for r in range(N):
        for y in range(B):
            for x in range(1, G, 2):
                ref = buf_a.at[x, y, r]
                pltpu.make_async_copy(ref, ref, xrecv.at[x, y, r]).wait()
    third = level_attend(2)

    a_end, b_end = plan.starts[1], plan.starts[2]

    def combine(levels):
        top = functools.reduce(jnp.maximum, [lse for _, lse in levels])
        shares = [jnp.exp(lse - top) for _, lse in levels]
        return sum(s * o for s, (o, _) in zip(shares, levels)) / sum(shares)

    base, slot = plan.source(lax.broadcasted_iota(jnp.int32, (plan.rows, R), 1))
    token = lax.broadcasted_iota(jnp.int32, (plan.rows, R), 0)
    out_lane = lax.broadcasted_iota(jnp.int32, (plan.rows, LANES), 1)
    attention = []
    for c in range(CHUNKS):
        (o1, l1), (o2, l2), (o3, l3) = first[c], second[c], third[c]
        mixed = jnp.concatenate(
            [
                combine([(o1[:a_end], l1[:a_end]), (o2[:a_end], l2[:a_end]), (o3, l3)]),
                combine([(o1[a_end:b_end], l1[a_end:b_end]), (o2[a_end:], l2[a_end:])]),
                o1[b_end:],
            ],
            axis=0,
        ).astype(jnp.bfloat16)
        back = []
        for half in range(2):
            hit = token == base + ((slot + offs_ref[1, 2 * c + half]) & (plan.period - 1))
            onehot = jnp.where(hit, jnp.float32(1), jnp.float32(0)).astype(jnp.bfloat16)
            back.append(jnp.dot(onehot, mixed, preferred_element_type=jnp.float32))
        attention.append(jnp.where(out_lane < HD, back[0], back[1]).astype(jnp.bfloat16))
    attention = jnp.concatenate(attention, axis=1)
    o_ref[...] = jnp.dot(attention, w_ref[...], preferred_element_type=jnp.float32).astype(o_ref.dtype)

    for part in range(3):
        for r in range(N):
            goes_left = si > 0 if r == 0 else (si > 0) & (si + r <= N - 1)
            goes_right = si < N - 1 if r == 0 else (si < N - 1) & (si + r > N - 1)

            @pl.when(goes_left)
            def _():
                zcopy(part, r, 0).wait_send()

            @pl.when(goes_right)
            def _():
                zcopy(part, r, 1).wait_send()

            if part < 2:
                for step in range(1, B):
                    ycopy(part, r, step).wait_send()
            if part == 0:
                for y in range(B):
                    for step in range(1, G // 2):
                        xcopy(y, r, step).wait_send()
                    for x in range(0, G, 2):
                        fcopy(x, y, r).wait_send()


def solution(mesh):
    G, B, N = mesh.shape["grp"], mesh.shape["blk"], mesh.shape["set"]

    def per_device(queries, keys, values, valid, offsets, w_out):
        rows, width = queries.shape
        plan = Plan(G, B, N, rows)
        vmem = pl.BlockSpec(memory_space=pltpu.VMEM)
        smem = pl.BlockSpec(memory_space=pltpu.SMEM)
        dma = pltpu.SemaphoreType.DMA
        ra, rb, rc = plan.sizes
        return pl.pallas_call(
            functools.partial(kernel, plan),
            out_shape=jax.ShapeDtypeStruct((rows, w_out.shape[1]), jnp.bfloat16),
            in_specs=[vmem, vmem, vmem, vmem, smem, vmem],
            out_specs=vmem,
            scratch_shapes=[
                pltpu.VMEM((G, B, N, 2 * CHUNKS + 1, ra, LANES), jnp.bfloat16),
                pltpu.VMEM((B, N, 2 * CHUNKS, rb, LANES), jnp.bfloat16),
                pltpu.VMEM((N, 2 * CHUNKS, rc, LANES), jnp.bfloat16),
                pltpu.VMEM((CHUNKS, plan.total, LANES), jnp.bfloat16),
                dma((3, N)),
                dma((3, N, 2)),
                dma((2, B, N)),
                dma((2, B, N)),
                dma((G, B, N)),
                dma((G // 2, B, N)),
                dma((G, B, N)),
            ],
            compiler_params=pltpu.CompilerParams(
                collective_id=0, has_side_effects=True, vmem_limit_bytes=60 * 1024 * 1024
            ),
        )(queries, keys, values, valid.reshape(1, rows), offsets, w_out)

    rows_spec = P(("grp", "blk", "set"), None)
    return jax.shard_map(
        per_device,
        mesh=mesh,
        in_specs=(rows_spec, rows_spec, rows_spec, P(("grp", "blk", "set")), P(), P()),
        out_specs=rows_spec,
        check_vma=False,
    )
```

time: 112 us -> 30.6 us (0.27)
  blocking collectives: 77.7 us -> 0 us
  Pallas kernels: 0 us -> 28.8 us
  local copies, waits for them, and re-layouts: 15.7 us -> 1.62 us
  matrix products: 9.82 us -> 0 us
  other arithmetic: 7.34 us -> 0 us
    all_gather x9 -> x0, blocking collectives: 77.7 us -> none  [the longest x1 14.4 us: per_device(): lax.all_gather(values, 'set', axis=0, tiled=True)]
    pallas_call x0 -> x1, Pallas kernels: none -> 28.8 us  [per_device(): pl.pallas_call(functools.partial(kernel, plan), out_shape=jax.ShapeDtypeS...]
    dot_general x37 -> x0, matrix products: 9.82 us -> none  [the longest x18 4.82 us: head_attend(): lax.dot_general(query_head, key_head, (((1,), (1,)), ((), ())), preferred...]
    reduce_sum x24 -> x0, other arithmetic: 6.67 us -> none  [the longest x18 3.53 us: head_attend(): totals = jnp.sum(weights, axis=1)]
    reshape x9 -> x0, local copies, waits for them, and re-layouts: 4.44 us -> none  [the longest x6 2.57 us: pick_rows(): matrix.reshape(row_total // cycle_length, cycle_length, HEAD_COUNT, HD)]
    unnamed x33 -> x1, local copies, waits for them, and re-layouts: 4.55 us -> 1.62 us
    reduce_sum x4 -> x0, local copies, waits for them, and re-layouts: 1.92 us -> none  [pick_rows(): jnp.sum(jnp.where(selector[None, :, :, None], blocks, jnp.zeros((), matri...]
    all_gather x4 -> x0, local copies, waits for them, and re-layouts: 1.55 us -> none  [the longest x1 0.91 us: per_device(): lax.all_gather(keys, 'set', axis=0, tiled=True)]
where the time goes in v1:
time: 30.6 us; the launch traced here: 30.4 us
  Pallas kernels  28.8 us (94%)
  local copies, waits for them, and re-layouts  1.62 us (5%)
    pallas_call x1, Pallas kernels, per_device(): pl.pallas_call(functools.partial(kernel, plan), out_shape=jax.ShapeDtypeS...  28.8 us
    unnamed x1, local copies, waits for them, and re-layouts  1.62 us

profile of v1, /device:TPU:0, one launch (start us, length us, event | category | flops | bytes accessed | tf_op | source)
XLA Modules:
  0.0 30.4 jit_solution(17619696472153112783)
XLA Ops:
  0.0 28.8 %shard_map.64 = bf16[128,768]{1,0:T(8,128)(2,1)} custom-call(bf16[128,384]{1,0:T(8,128)(2,1)} %q_ref.1, bf16[128,384]{1,0:T(8,128)(2,1)} %k_ref.1, bf16[128,384]{1,0:T(8,128)(2,1)} %v_ref.1, s32[1,128]{1,0:T(1,128)} %bitcast.1, s32[2,6]{1,0:T(2,128)} %offs_ref.1, bf16[384,768]{1,0:T(8,128)(2,1)} %w_ref.1), custom_call_target="tpu_custom_call" | custom-call | tf_op jit(solution)/shard_map/pallas_call | solution.py:379
  28.8 1.6 %copy.8 = bf16[128,768]{1,0:T(8,128)(2,1)} copy(bf16[128,768]{1,0:T(8,128)(2,1)} %shard_map.64) | data formatting | bytes 393216

commit v2 on v1

v2 whole, which is shorter than its diff:
```python
import functools

import jax
import jax.numpy as jnp
from jax import lax
from jax.experimental import pallas as pl
from jax.experimental.pallas import tpu as pltpu
from jax.sharding import PartitionSpec as P

HEAD_COUNT = 6
HD = 64
LANES = 128
UNIT = 16
FLAG_STRIDE = 8
CHUNKS = HEAD_COUNT * HD // LANES
MESH = pl.DeviceIdType.MESH
NEG = -1e30
FLAG_SPOT = 2 * CHUNKS - 2


def spot(at):
    return at if at < FLAG_SPOT else at + 1


def units(count):
    return -(-count // UNIT)


def split_pow2(x, size):
    shift = size.bit_length() - 1
    return lax.shift_right_logical(x, shift), x & (size - 1)


class Plan:
    def __init__(self, grp, blk, n, rows):
        self.grp, self.blk, self.n, self.rows = grp, blk, n, rows
        self.period = grp * blk
        self.c3 = rows // self.period
        c2 = rows // blk
        self.counts = (self.c3, c2 - self.c3, rows - c2)
        self.units = tuple(units(c) for c in self.counts)
        self.sizes = tuple(u * UNIT for u in self.units)
        self.starts = (0, self.sizes[0], self.sizes[0] + self.sizes[1])
        self.total = sum(self.sizes)

    def source(self, t):
        a = t
        b = t - self.starts[1]
        c = t - self.starts[2]
        bv, bg = split_pow2(b, self.c3)
        cv, cg = split_pow2(c, self.c3)
        ck, cm = split_pow2(cv, self.grp)
        is_a = t < self.starts[1]
        is_b = t < self.starts[2]
        group = jnp.where(is_a, a, jnp.where(is_b, bg, cg))
        slot = jnp.where(is_a, 0, jnp.where(is_b, (bv + 1) * self.blk, cm * self.blk + ck + 1))
        local = jnp.where(is_a, a, jnp.where(is_b, b, c))
        count = jnp.where(is_a, self.counts[0], jnp.where(is_b, self.counts[1], self.counts[2]))
        return jnp.where(local < count, group * self.period, -(1 << 20)), slot


def kernel(
    plan, q_ref, k_ref, v_ref, valid_ref, offs_ref, o_ref,
    buf_a, buf_b, buf_c, qs, qdel, mixes, lses, comb, cdel,
    zrecv, zsend, yrecv, ysend, xrecv, xsend, fsend, dsend, drecv,
):
    G, B, N = plan.grp, plan.blk, plan.n
    R = plan.total
    gi, bi, si = lax.axis_index("grp"), lax.axis_index("blk"), lax.axis_index("set")
    core = gi % 2
    partner = gi + 1 - 2 * core
    is_first, is_last = si == 0, si == N - 1
    is_end = is_first | is_last
    is_helper = (si == 1) | (si == N - 2)
    helper_of_end = jnp.where(is_first, 1, N - 2)
    end_of_helper = jnp.where(si == 1, 0, N - 1)

    def cases(condition, action):
        pl.when(condition)(lambda: action(True))
        pl.when(jnp.logical_not(condition))(lambda: action(False))

    def peer_grp(step):
        return lax.rem(gi + 2 * step, G)

    barrier = pltpu.get_barrier_semaphore()

    def greet(g, b, s):
        pl.semaphore_signal(barrier, inc=1, device_id=(g, b, s), device_id_type=MESH)

    @pl.when(si > 0)
    def _():
        greet(gi, bi, si - 1)

    @pl.when(si < N - 1)
    def _():
        greet(gi, bi, si + 1)

    for step in range(1, B):
        greet(gi, lax.rem(bi + step, B), si)
    for step in range(1, G // 2):
        greet(peer_grp(step), bi, si)
    greet(partner, bi, si)

    lane = lax.broadcasted_iota(jnp.int32, (R, LANES), 1)
    base, slot = plan.source(lax.broadcasted_iota(jnp.int32, (R, plan.rows), 0))
    token = lax.broadcasted_iota(jnp.int32, (R, plan.rows), 1)
    valid_row = (valid_ref[...] > 0).astype(jnp.float32)
    flag_lane = lax.broadcasted_iota(jnp.int32, (UNIT, LANES), 1)
    flags = jnp.zeros((UNIT, LANES), jnp.float32)
    for c in range(CHUNKS):
        cols = slice(c * LANES, (c + 1) * LANES)
        packed = jnp.concatenate([q_ref[:, cols], k_ref[:, cols], v_ref[:, cols]], axis=1)
        moved = []
        for half in range(2):
            h = 2 * c + half
            hit = token == base + ((slot + offs_ref[1, h]) & (plan.period - 1))
            onehot = jnp.where(hit, jnp.float32(1), jnp.float32(0))
            moved.append(jnp.dot(onehot.astype(jnp.bfloat16), packed, preferred_element_type=jnp.float32))
            column = jnp.sum(onehot * valid_row, axis=1, keepdims=True)
            for u in range(R // UNIT):
                flags = jnp.where(
                    flag_lane == u * FLAG_STRIDE + h, column[u * UNIT:(u + 1) * UNIT, :], flags
                )
        for part in range(3):
            seg = slice(part * LANES, (part + 1) * LANES)
            got = jnp.where(lane < HD, moved[0][:, seg], moved[1][:, seg])
            if part == 0:
                qs[c] = (got * 0.125).astype(jnp.bfloat16)
                continue
            got = got.astype(jnp.bfloat16)
            at = 2 * c + part - 1
            buf_a[0, 0, 0, spot(at)] = got[:plan.starts[1]]
            buf_b[0, 0, at] = got[plan.starts[1]:plan.starts[2]]
            buf_c[0, at] = got[plan.starts[2]:]
    buf_a[0, 0, 0, FLAG_SPOT, 0:UNIT] = flags.astype(jnp.bfloat16)

    left_side = jnp.where(si > 0, 1, 0)
    right_side = jnp.where(si < N - 1, 1, 0)
    pl.semaphore_wait(barrier, left_side + right_side + (B - 1) + (G // 2 - 1) + 1)

    def width(part, short):
        full = 2 * CHUNKS + (part == 0)
        return pl.ds(0, full - 2 if short else full)

    def zslot(part, r, short):
        w = width(part, short)
        return (buf_a.at[0, 0], buf_b.at[0], buf_c)[part].at[r, w]

    def zcopy(part, r, direction, short):
        to = (r + 1) % N if direction == 0 else (r - 1) % N
        near = si - 1 if direction == 0 else si + 1
        return pltpu.make_async_remote_copy(
            src_ref=zslot(part, r, short), dst_ref=zslot(part, to, short),
            send_sem=zsend.at[part, r, direction], recv_sem=zrecv.at[part, to],
            device_id=(gi, bi, near), device_id_type=MESH,
        )

    def to_near(part, r, direction, method):
        near_end = si == 1 if direction == 0 else si == N - 2
        cases(near_end, lambda short: getattr(zcopy(part, r, direction, short), method)())

    def yplace(part, x, r, short):
        w = width(part, short)
        return buf_a.at[0, x, r, w] if part == 0 else buf_b.at[x, r, w]

    def ycopy(part, r, step, short):
        to = B - step
        return pltpu.make_async_remote_copy(
            src_ref=yplace(part, 0, r, short), dst_ref=yplace(part, to, r, short),
            send_sem=ysend.at[part, step, r], recv_sem=yrecv.at[part, to, r],
            device_id=(gi, lax.rem(bi + step, B), si), device_id_type=MESH,
        )

    def xplace(x, y, r, short):
        return buf_a.at[x, y, r, width(0, short)]

    def xcopy(y, r, step, short):
        to = (2 * (G // 2 - step)) % G
        return pltpu.make_async_remote_copy(
            src_ref=xplace(0, y, r, short), dst_ref=xplace(to, y, r, short),
            send_sem=xsend.at[step, y, r], recv_sem=xrecv.at[to, y, r],
            device_id=(peer_grp(step), bi, si), device_id_type=MESH,
        )

    def fcopy(x, y, r, short):
        return pltpu.make_async_remote_copy(
            src_ref=xplace(x, y, r, short), dst_ref=xplace(x + 1, y, r, short),
            send_sem=fsend.at[x, y, r], recv_sem=xrecv.at[x + 1, y, r],
            device_id=(partner, bi, si), device_id_type=MESH,
        )

    def qcopy():
        return pltpu.make_async_remote_copy(
            src_ref=qs.at[CHUNKS - 1], dst_ref=qdel, send_sem=dsend.at[0], recv_sem=drecv.at[0],
            device_id=(gi, bi, helper_of_end), device_id_type=MESH,
        )

    def backcopy():
        return pltpu.make_async_remote_copy(
            src_ref=cdel, dst_ref=comb.at[CHUNKS - 1], send_sem=dsend.at[1], recv_sem=drecv.at[1],
            device_id=(gi, bi, end_of_helper), device_id_type=MESH,
        )

    def wait_for(ref, sem):
        pltpu.make_async_copy(ref, ref, sem).wait()

    def spread_grp(y, r, short):
        for step in range(1, G // 2):
            xcopy(y, r, step, short).start()
        fcopy(0, y, r, short).start()

    def spread_blk(part, r, short):
        for step in range(1, B):
            ycopy(part, r, step, short).start()

    def spread(part, r):
        def action(short):
            if part < 2:
                spread_blk(part, r, short)
            if part == 0:
                spread_grp(0, r, short)

        cases(is_end, action)

    def own_z(part):
        pl.when(si > 0)(lambda: to_near(part, 0, 0, "start"))
        pl.when(si < N - 1)(lambda: to_near(part, 0, 1, "start"))

    def arrive(part, r):
        cases(is_end, lambda short: wait_for(zslot(part, r, short), zrecv.at[part, r]))

    def take(part, d):
        @pl.when(si + d <= N - 1)
        def _():
            arrive(part, d)
            pl.when(si > 0)(lambda: to_near(part, d, 0, "start"))
            if part < 2:
                spread(part, d)

        @pl.when(si - d >= 0)
        def _():
            arrive(part, N - d)
            pl.when(si < N - 1)(lambda: to_near(part, N - d, 1, "start"))
            if part < 2:
                spread(part, N - d)

    own_z(0)
    spread(0, 0)
    own_z(1)
    spread(1, 0)
    pl.when(is_end)(lambda: qcopy().start())
    for d in range(1, N):
        take(0, d)
        if d == 2:
            own_z(2)
        take(1, d)

    def relay_y(short):
        for r in range(N):
            for y in range(1, B):
                wait_for(yplace(0, y, r, short), yrecv.at[0, y, r])
                spread_grp(y, r, short)

    def relay_x(short):
        for r in range(N):
            for y in range(B):
                for step in range(1, G // 2):
                    wait_for(xplace(2 * step, y, r, short), xrecv.at[2 * step, y, r])
                    fcopy(2 * step, y, r, short).start()

    def last_x(short):
        for r in range(N):
            for y in range(B):
                for x in range(1, G, 2):
                    wait_for(xplace(x, y, r, short), xrecv.at[x, y, r])

    def last_y(short):
        for r in range(N):
            for y in range(1, B):
                wait_for(yplace(1, y, r, short), yrecv.at[1, y, r])

    cases(is_end, relay_y)
    take(2, 1)
    cases(is_end, relay_x)
    for d in range(2, N - 1):
        take(2, d)

    head_pick = lax.broadcasted_iota(jnp.int32, (FLAG_STRIDE, LANES), 1) & (FLAG_STRIDE - 1)
    head_pick = head_pick == lax.broadcasted_iota(jnp.int32, (FLAG_STRIDE, LANES), 0)
    head_pick = jnp.where(head_pick, jnp.float32(1), jnp.float32(0)).astype(jnp.bfloat16)

    def gather(level, at):
        pieces = []
        for u in range(plan.units[0]):
            rows = slice(u * UNIT, (u + 1) * UNIT)
            at_a = spot(at)
            part = (buf_a[0, 0, :, at_a, rows], buf_a[0, :, :, at_a, rows], buf_a[:, :, :, at_a, rows])[level]
            pieces.append(part.reshape(-1, LANES))
        if level < 2:
            for u in range(plan.units[1]):
                rows = slice(u * UNIT, (u + 1) * UNIT)
                part = buf_b[0, :, at, rows] if level == 0 else buf_b[:, :, at, rows]
                pieces.append(part.reshape(-1, LANES))
        if level == 0:
            for u in range(plan.units[2]):
                pieces.append(buf_c[:, at, u * UNIT:(u + 1) * UNIT].reshape(-1, LANES))
        return pieces[0] if len(pieces) == 1 else jnp.concatenate(pieces, axis=0)

    def level_attend(level):
        M = (R, plan.starts[2], plan.starts[1])[level]
        tiles = M // UNIT
        devices = (N, B * N, G * B * N)[level]
        per_unit = devices * UNIT
        rows = slice(0, UNIT)
        at = FLAG_SPOT
        tall = (buf_a[0, 0, :, at, rows], buf_a[0, :, :, at, rows], buf_a[:, :, :, at, rows])[level]
        tall = tall.reshape(per_unit, LANES).astype(jnp.float32)
        unit_lane = lax.broadcasted_iota(jnp.int32, (per_unit, LANES), 1) // FLAG_STRIDE
        tall = [jnp.where(unit_lane == u, tall, 0.0).astype(jnp.bfloat16) for u in range(tiles)]
        tall = tall[0] if tiles == 1 else jnp.concatenate(tall, axis=0)
        ok = lax.dot_general(
            head_pick, tall, (((1,), (1,)), ((), ())), preferred_element_type=jnp.float32
        )
        keys = per_unit * tiles
        t = lax.broadcasted_iota(jnp.int32, (M, keys), 0)
        key = lax.broadcasted_iota(jnp.int32, (M, keys), 1)
        home = (t // UNIT) * per_unit + (t % UNIT)
        half_lane = lax.broadcasted_iota(jnp.int32, (M, LANES), 1) < HD

        def job(index):
            c = min(index, CHUNKS - 1)
            q = qs[c, 0:M] if index < CHUNKS else qdel[0:M]
            own = key == (home if index < CHUNKS else home + end_slot * UNIT)
            zero = jnp.zeros_like(q)
            both = jnp.concatenate([jnp.where(half_lane, q, zero), jnp.where(half_lane, zero, q)], axis=0)
            scores = lax.dot_general(
                both, gather(level, 2 * c), (((1,), (1,)), ((), ())), preferred_element_type=jnp.float32
            )
            values = gather(level, 2 * c + 1)
            probs, tops, totals = [], [], []
            for half in range(2):
                h = 2 * c + half
                s = jnp.where(own | (ok[h:h + 1, :] > 0.5), scores[half * M:(half + 1) * M], NEG)
                top = jnp.max(s, axis=1, keepdims=True)
                weight = jnp.exp(s - top)
                totals.append(jnp.sum(weight, axis=1, keepdims=True))
                tops.append(top)
                probs.append(weight.astype(jnp.bfloat16))
            mixed = jnp.dot(jnp.concatenate(probs, axis=0), values, preferred_element_type=jnp.float32)
            mixes[level, index, 0:M] = jnp.where(half_lane, mixed[:M] / totals[0], mixed[M:] / totals[1])
            lses[level, index, 0:M] = jnp.where(
                half_lane, tops[0] + jnp.log(totals[0]), tops[1] + jnp.log(totals[1])
            )

        return job

    a_end, b_end = plan.starts[1], plan.starts[2]

    def combine(levels):
        top = functools.reduce(jnp.maximum, [lse for _, lse in levels])
        shares = [jnp.exp(lse - top) for _, lse in levels]
        return sum(s * o for s, (o, _) in zip(shares, levels)) / sum(shares)

    end_slot = jnp.where(si == 1, N - 1, 1)

    def level_jobs(level):
        job = level_attend(level)
        pl.when(is_helper)(lambda: job(CHUNKS))
        if level == 1:
            @pl.when(is_helper)
            def _():
                cdel[...] = merged(CHUNKS)
                backcopy().start()
        for c in range(CHUNKS - 1):
            job(c)
        pl.when(jnp.logical_not(is_end))(lambda: job(CHUNKS - 1))

    def merged(index):
        o1, o2, o3 = (mixes.at[level, index] for level in range(3))
        l1, l2, l3 = (lses.at[level, index] for level in range(3))
        a, b, c = slice(0, a_end), slice(a_end, b_end), slice(b_end, R)
        return jnp.concatenate(
            [
                combine([(o1[a], l1[a]), (o2[a], l2[a]), (o3[a], l3[a])]),
                combine([(o1[b], l1[b]), (o2[b], l2[b])]),
                o1[c],
            ],
            axis=0,
        ).astype(jnp.bfloat16)

    cases(is_end, last_x)
    pl.when(is_helper)(lambda: wait_for(qdel, drecv.at[0]))
    level_jobs(2)
    take(2, N - 1)
    level_jobs(0)
    cases(is_end, last_y)
    level_jobs(1)

    for c in range(CHUNKS - 1):
        comb[c] = merged(c)

    @pl.when(jnp.logical_not(is_end))
    def _():
        comb[CHUNKS - 1] = merged(CHUNKS - 1)

    pl.when(is_end)(lambda: wait_for(comb.at[CHUNKS - 1], drecv.at[1]))

    base, slot = plan.source(lax.broadcasted_iota(jnp.int32, (plan.rows, R), 1))
    token = lax.broadcasted_iota(jnp.int32, (plan.rows, R), 0)
    out_lane = lax.broadcasted_iota(jnp.int32, (plan.rows, LANES), 1)
    for c in range(CHUNKS):
        mixed = comb[c]
        back = []
        for half in range(2):
            hit = token == base + ((slot + offs_ref[1, 2 * c + half]) & (plan.period - 1))
            onehot = jnp.where(hit, jnp.float32(1), jnp.float32(0)).astype(jnp.bfloat16)
            back.append(jnp.dot(onehot, mixed, preferred_element_type=jnp.float32))
        o_ref[:, c * LANES:(c + 1) * LANES] = jnp.where(out_lane < HD, back[0], back[1]).astype(o_ref.dtype)

    def sent(short):
        for r in range(N):
            for step in range(1, B):
                ycopy(0, r, step, short).wait_send()
                ycopy(1, r, step, short).wait_send()
            for y in range(B):
                for step in range(1, G // 2):
                    xcopy(y, r, step, short).wait_send()
                for x in range(0, G, 2):
                    fcopy(x, y, r, short).wait_send()

    cases(is_end, sent)
    pl.when(is_end)(lambda: qcopy().wait_send())
    pl.when(is_helper)(lambda: backcopy().wait_send())
    for part in range(3):
        for r in range(N):
            goes_left = si > 0 if r == 0 else (si > 0) & (si + r <= N - 1)
            goes_right = si < N - 1 if r == 0 else (si < N - 1) & (si + r > N - 1)
            pl.when(goes_left)(lambda: to_near(part, r, 0, "wait_send"))
            pl.when(goes_right)(lambda: to_near(part, r, 1, "wait_send"))


def solution(mesh):
    G, B, N = mesh.shape["grp"], mesh.shape["blk"], mesh.shape["set"]

    def per_device(queries, keys, values, valid, offsets, w_out):
        rows, width = queries.shape
        plan = Plan(G, B, N, rows)
        vmem = pl.BlockSpec(memory_space=pltpu.VMEM)
        smem = pl.BlockSpec(memory_space=pltpu.SMEM)
        dma = pltpu.SemaphoreType.DMA
        ra, rb, rc = plan.sizes
        attention = pl.pallas_call(
            functools.partial(kernel, plan),
            out_shape=jax.ShapeDtypeStruct((rows, width), jnp.bfloat16),
            in_specs=[vmem, vmem, vmem, vmem, smem],
            out_specs=vmem,
            scratch_shapes=[
                pltpu.VMEM((G, B, N, 2 * CHUNKS + 1, ra, LANES), jnp.bfloat16),
                pltpu.VMEM((B, N, 2 * CHUNKS, rb, LANES), jnp.bfloat16),
                pltpu.VMEM((N, 2 * CHUNKS, rc, LANES), jnp.bfloat16),
                pltpu.VMEM((CHUNKS, plan.total, LANES), jnp.bfloat16),
                pltpu.VMEM((plan.total, LANES), jnp.bfloat16),
                pltpu.VMEM((3, CHUNKS + 1, plan.total, LANES), jnp.float32),
                pltpu.VMEM((3, CHUNKS + 1, plan.total, LANES), jnp.float32),
                pltpu.VMEM((CHUNKS, plan.total, LANES), jnp.bfloat16),
                pltpu.VMEM((plan.total, LANES), jnp.bfloat16),
                dma((3, N)),
                dma((3, N, 2)),
                dma((2, B, N)),
                dma((2, B, N)),
                dma((G, B, N)),
                dma((G // 2, B, N)),
                dma((G, B, N)),
                dma((2,)),
                dma((2,)),
            ],
            compiler_params=pltpu.CompilerParams(
                collective_id=0, has_side_effects=True, vmem_limit_bytes=60 * 1024 * 1024
            ),
        )(queries, keys, values, valid.reshape(1, rows), offsets)
        return jnp.dot(attention, w_out, preferred_element_type=jnp.float32).astype(jnp.bfloat16)

    rows_spec = P(("grp", "blk", "set"), None)
    return jax.shard_map(
        per_device,
        mesh=mesh,
        in_specs=(rows_spec, rows_spec, rows_spec, P(("grp", "blk", "set")), P(), P()),
        out_specs=rows_spec,
        check_vma=False,
    )
```

time: 30.6 us -> 31 us (1.013)
  matrix products: 0 us -> 1.84 us
  local copies, waits for them, and re-layouts: 1.62 us -> 0.01 us
    dot_general x0 -> x1, matrix products: none -> 1.84 us  [per_device(): jnp.dot(attention, w_out, preferred_element_type=jnp.float32)]
    unnamed x1 -> x2, local copies, waits for them, and re-layouts: 1.62 us -> 0.01 us
where the time goes in v2:
time: 31 us; the launch traced here: 30.9 us
  Pallas kernels  29 us (94%)
  matrix products  1.84 us (6%)
    pallas_call x1, Pallas kernels, per_device(): pl.pallas_call(functools.partial(kernel, plan), out_shape=jax.ShapeDtypeS...  29 us
    dot_general x1, matrix products, per_device(): jnp.dot(attention, w_out, preferred_element_type=jnp.float32)  1.84 us

profile of v2, /device:TPU:0, one launch (start us, length us, event | category | flops | bytes accessed | tf_op | source)
XLA Modules:
  0.0 30.9 jit_solution(10825611113127420467)
XLA Ops:
  0.0 0.0 copy-start
  0.0 29.0 %shard_map.64 = bf16[128,384]{1,0:T(8,128)(2,1)} custom-call(bf16[128,384]{1,0:T(8,128)(2,1)} %q_ref.1, bf16[128,384]{1,0:T(8,128)(2,1)} %k_ref.1, bf16[128,384]{1,0:T(8,128)(2,1)} %v_ref.1, s32[1,128]{1,0:T(1,128)} %bitcast.3, s32[2,6]{1,0:T(2,128)} %offs_ref.1), custom_call_target="tpu_custom_call" | custom-call | tf_op jit(solution)/shard_map/pallas_call | solution.py:452
  29.0 0.0 copy-done
  29.0 1.8 %convolution_convert_fusion = bf16[128,768]{1,0:T(8,128)(2,1)} fusion(bf16[128,384]{1,0:T(8,128)(2,1)} %shard_map.64, bf16[384,768]{1,0:T(8,128)(2,1)S(1)} %copy-done), kind=kOutput, calls=%fused_computation | convolution fusion | flops 75595776 | bytes 884736 | tf_op jit(solution)/shard_map/dot_general | solution.py:481
Async XLA Ops:
  0.0 29.0 %copy-start = (bf16[384,768]{1,0:T(8,128)(2,1)S(1)}, bf16[384,768]{1,0:T(8,128)(2,1)}, u32[]{:S(2)}) copy-start(bf16[384,768]{1,0:T(8,128)(2,1)} %param.11) | copy-start | bytes 1769476
